TPU v7x, 32 devices: a whole 2x2x4 slice. The times are simulated.
32 devices in a mesh: section: 4 (over y, core), dp: 2 (over x), tensor: 4 (over z).
Axes of the slice: x: 2, y: 2, z: 4, core: 2. Of those that a mesh axis runs over, the one named last changes fastest.
Arguments:
- shadow_weight_copy: bfloat16 [4, 4096, 4096], P('section', None, 'tensor'), may hold values from -6 to 6
- newest_weight_version: bfloat16 [4, 4096, 4096], P('section', 'dp', 'tensor'), may hold values from -6 to 6
- momentum: bfloat16 [4, 4096, 4096], P('section', 'dp', 'tensor'), may hold values from -3 to 3
- pending_section_input: bfloat16 [2, 4, 64, 4096], P('dp', 'section', None, 'tensor'), may hold values from -16 to 16
- incoming_micro_input: bfloat16 [2, 3, 64, 4096], P('dp', None, None, 'tensor'), may hold values from -16 to 16
- pending_output_gradient: bfloat16 [2, 4, 64, 4096], P('dp', 'section', None, 'tensor'), may hold values from -16 to 16
- loss_gradient_rows: bfloat16 [2, 3, 64, 4096], P('dp', None, None, 'tensor'), may hold values from -16 to 16
- stashed: bfloat16 [2, 4, 4, 64, 4096], P('dp', 'section', None, None, 'tensor'), may hold values from -16 to 16
Outputs:
- forward_out: bfloat16 [2, 4, 4, 64, 4096], P('dp', 'section', None, None, 'tensor')
- backward_out: bfloat16 [2, 4, 4, 64, 4096], P('dp', 'section', None, None, 'tensor')
- w_next: bfloat16 [4, 4096, 4096], P('section', 'dp', 'tensor')
- m_next: bfloat16 [4, 4096, 4096], P('section', 'dp', 'tensor')
All inputs are finite; a program needn't handle non-finite values.
Results may differ from a plain program's by a relative error of at most 0.025.
Values may be sent and summed in bfloat16 or wider, within the bound.
A program may use at most 128 MiB of HBM per device.

v0:
```python
import math

import jax
import jax.numpy as jnp
from jax import lax
from jax.sharding import PartitionSpec as P

EPSILON = 1e-06
MOMENTUM_RATE = 0.9
LEARNING_RATE = 0.05


def shifted(block, axis, distance):
    devices = range(lax.axis_size(axis))
    route = [(i - distance, i) for i in devices if i - distance in devices]
    return lax.ppermute(block, axis, route)


def normalized(values):
    factor = lax.rsqrt(jnp.mean(values * values, axis=-1, keepdims=True) + EPSILON)
    return (values * factor, factor)


def body(
    shadow_weight_copy,
    newest_weight_version,
    momentum,
    pending_section_input,
    incoming_micro_input,
    pending_output_gradient,
    loss_gradient_rows,
    stashed,
):
    weight = shadow_weight_copy[0]
    extent = weight.shape[0]
    own_cols = weight.shape[1]
    root_width = math.sqrt(extent)
    tick_count = stashed.shape[2]
    section_count = lax.axis_size("section")
    is_first = lax.axis_index("section") == 0
    is_last = lax.axis_index("section") == section_count - 1
    col_start = lax.axis_index("tensor") * own_cols
    current_input = pending_section_input[0, 0]
    current_gradient = pending_output_gradient[0, 0]
    forward_list = []
    backward_list = []
    kept_list = []
    grad_list = []
    for tick_index in range(tick_count):
        if tick_index > 0:
            from_below = shifted(forward_list[-1], "section", 1)
            current_input = jnp.where(is_first, incoming_micro_input[0, tick_index - 1], from_below)
            from_above = shifted(backward_list[-1], "section", -1)
            current_gradient = jnp.where(is_last, loss_gradient_rows[0, tick_index - 1], from_above)
        whole_x, whole_kept = (
            lax.all_gather(current_input, "tensor", axis=1, tiled=True),
            lax.all_gather(stashed[0, 0, tick_index], "tensor", axis=1, tiled=True),
        )
        x_hat, unused = normalized(whole_x.astype(jnp.float32))
        branch = (
            jnp.dot(x_hat.astype(jnp.bfloat16), weight, preferred_element_type=jnp.float32)
            / root_width
        )
        forward_list.append((current_input.astype(jnp.float32) + branch).astype(jnp.bfloat16))
        kept_hat, kept_factor = normalized(whole_kept.astype(jnp.float32))
        partial_value = (
            lax.dot_general(
                current_gradient,
                weight,
                (((1,), (1,)), ((), ())),
                preferred_element_type=jnp.float32,
            )
            / root_width
        ).astype(jnp.bfloat16)
        own_hat = lax.dynamic_slice_in_dim(kept_hat, col_start, own_cols, 1)
        own_grad = lax.psum_scatter(
            partial_value, "tensor", scatter_dimension=1, tiled=True
        ).astype(jnp.float32)
        inner_dot = lax.psum(jnp.sum(own_grad * own_hat, axis=-1, keepdims=True), "tensor") / extent
        input_grad = (
            current_gradient.astype(jnp.float32) + (own_grad - own_hat * inner_dot) * kept_factor
        )
        backward_list.append(input_grad.astype(jnp.bfloat16))
        kept_list.append(kept_hat.astype(jnp.bfloat16))
        grad_list.append(current_gradient)
    kept_rows = jnp.concatenate(kept_list, axis=0)
    grad_rows = jnp.concatenate(grad_list, axis=0)
    replica_term = (
        lax.dot_general(
            kept_rows, grad_rows, (((0,), (0,)), ((), ())), preferred_element_type=jnp.float32
        )
        / root_width
    ).astype(jnp.bfloat16)
    summed = lax.psum_scatter(replica_term, "dp", scatter_dimension=0, tiled=True).astype(
        jnp.float32
    )
    velocity = MOMENTUM_RATE * momentum[0].astype(jnp.float32) + summed
    w_next = (newest_weight_version[0].astype(jnp.float32) - LEARNING_RATE * velocity).astype(
        jnp.bfloat16
    )[None]
    m_next = velocity.astype(jnp.bfloat16)[None]
    forward_out = jnp.stack(forward_list, axis=0)[None, None]
    backward_out = jnp.stack(backward_list, axis=0)[None, None]
    return (forward_out, backward_out, w_next, m_next)


def solution(mesh):
    return jax.shard_map(
        body,
        mesh=mesh,
        in_specs=(
            P("section", None, "tensor"),
            P("section", "dp", "tensor"),
            P("section", "dp", "tensor"),
            P("dp", "section", None, "tensor"),
            P("dp", None, None, "tensor"),
            P("dp", "section", None, "tensor"),
            P("dp", None, None, "tensor"),
            P("dp", "section", None, None, "tensor"),
        ),
        out_specs=(
            P("dp", "section", None, None, "tensor"),
            P("dp", "section", None, None, "tensor"),
            P("section", "dp", "tensor"),
            P("section", "dp", "tensor"),
        ),
        check_vma=False,
    )
```

profile of v0, /device:TPU:0, one launch (start us, length us, event | category | flops | bytes accessed | tf_op | source)
XLA Modules:
  0.0 335.9 jit_solution(7891010142634172775)
XLA Ops:
  7.2 7.0 %fusion.39 = bf16[64,4096]{1,0:T(8,128)(2,1)} fusion(bf16[1,4096,1024]{2,1,0:T(8,128)(2,1)} %param.8, bf16[1,1,64,1024]{3,2,1,0:T(8,128)(2,1)} %param.13), kind=kOutput, calls=%fused_computation.28 | convolution fusion | flops 537395200 | bytes 9043968 | tf_op jit(solution)/shard_map/dot_general | solution.py:67
  14.3 22.5 %all-gather.3 = bf16[1,1,1,64,4096]{4,3,2,1,0:T(8,128)(2,1)S(1)} all-gather(bf16[1,1,1,64,1024]{4,3,2,1,0:T(8,128)(2,1)S(1)} %get-tuple-element.14), channel_id=5, replica_groups=mesh['section'=4,'dp'=2,'tensor'=4] {'tensor'}, dimensions={4}, use_global_device_ids=true | all-gather | bytes 655360 | tf_op jit(solution)/shard_map/all_gather | solution.py:57
  37.1 15.9 %all-gather.1 = bf16[1,1,1,64,4096]{4,3,2,1,0:T(8,128)(2,1)S(1)} all-gather(bf16[1,1,1,64,1024]{4,3,2,1,0:T(8,128)(2,1)S(1)} %get-tuple-element.16), channel_id=3, replica_groups=mesh['section'=4,'dp'=2,'tensor'=4] {'tensor'}, dimensions={4}, use_global_device_ids=true | all-gather | bytes 655360 | tf_op jit(solution)/shard_map/all_gather | solution.py:57
  53.2 15.7 %all-gather.2 = bf16[1,1,1,64,4096]{4,3,2,1,0:T(8,128)(2,1)S(1)} all-gather(bf16[1,1,1,64,1024]{4,3,2,1,0:T(8,128)(2,1)S(1)} %get-tuple-element.15), channel_id=4, replica_groups=mesh['section'=4,'dp'=2,'tensor'=4] {'tensor'}, dimensions={4}, use_global_device_ids=true | all-gather | bytes 655360 | tf_op jit(solution)/shard_map/all_gather | solution.py:57
  70.2 9.0 %psum.28 = f32[64,1]{0,1:T(1,128)S(1)} all-reduce(f32[64,1]{0,1:T(1,128)S(1)} %bitcast.156), channel_id=1, replica_groups=mesh['section'=4,'dp'=2,'tensor'=4] {'tensor'}, use_global_device_ids=true, to_apply=%region_7.8 | all-reduce | flops 64 | bytes 512 | tf_op jit(solution)/shard_map/psum | solution.py:79
  80.2 1.3 collective-permute-start.3
  81.7 1.7 collective-permute-done.3
  84.4 6.8 %fusion.36 = bf16[64,4096]{1,0:T(8,128)(2,1)} fusion(bf16[64,1024]{1,0:T(8,128)(2,1)S(1)} %bitcast_select_fusion.2, bf16[1,4096,1024]{2,1,0:T(8,128)(2,1)} %param.8), kind=kOutput, calls=%fused_computation.27 | convolution fusion | flops 537395200 | bytes 9043968 | tf_op jit(solution)/shard_map/dot_general | solution.py:67
  92.3 21.8 %reduce-scatter.8.cloned.1.call-done = bf16[64,1024]{1,0:T(8,128)(2,1)} async-done(((bf16[64,4096]{1,0:T(8,128)(2,1)}), bf16[64,1024]{1,0:T(8,128)(2,1)}) %reduce-scatter.8.cloned.1.call-update) | async-done | bytes 131088 | tf_op jit(solution)/shard_map/reduce_scatter | solution.py:76
  115.2 8.6 %psum.29 = f32[64,1]{0,1:T(1,128)S(1)} all-reduce(f32[64,1]{0,1:T(1,128)S(1)} %bitcast.157), channel_id=1, replica_groups=mesh['section'=4,'dp'=2,'tensor'=4] {'tensor'}, use_global_device_ids=true, to_apply=%region_11.12 | all-reduce | flops 64 | bytes 512 | tf_op jit(solution)/shard_map/psum | solution.py:79
  124.9 1.3 collective-permute-start.4
  126.2 15.9 %all-gather.4 = bf16[1,1,1,64,4096]{4,3,2,1,0:T(8,128)(2,1)S(1)} all-gather(bf16[1,1,1,64,1024]{4,3,2,1,0:T(8,128)(2,1)S(1)} %get-tuple-element.17), channel_id=6, replica_groups=mesh['section'=4,'dp'=2,'tensor'=4] {'tensor'}, dimensions={4}, use_global_device_ids=true | all-gather | bytes 655360 | tf_op jit(solution)/shard_map/all_gather | solution.py:57
  143.0 6.8 %fusion.33 = bf16[64,4096]{1,0:T(8,128)(2,1)} fusion(bf16[64,1024]{1,0:T(8,128)(2,1)S(1)} %bitcast_select_fusion.1, bf16[1,4096,1024]{2,1,0:T(8,128)(2,1)} %param.8), kind=kOutput, calls=%fused_computation.26 | convolution fusion | flops 537395200 | bytes 9043968 | tf_op jit(solution)/shard_map/dot_general | solution.py:67
  151.1 21.0 %reduce-scatter.10.cloned.1.call-done = bf16[64,1024]{1,0:T(8,128)(2,1)} async-done(((bf16[64,4096]{1,0:T(8,128)(2,1)}), bf16[64,1024]{1,0:T(8,128)(2,1)}) %reduce-scatter.10.cloned.1.call-update) | async-done | bytes 131088 | tf_op jit(solution)/shard_map/reduce_scatter | solution.py:76
  173.1 8.6 %psum.30 = f32[64,1]{0,1:T(1,128)S(1)} all-reduce(f32[64,1]{0,1:T(1,128)S(1)} %bitcast.158), channel_id=1, replica_groups=mesh['section'=4,'dp'=2,'tensor'=4] {'tensor'}, use_global_device_ids=true, to_apply=%region_15.16 | all-reduce | flops 64 | bytes 512 | tf_op jit(solution)/shard_map/psum | solution.py:79
  184.1 1.9 collective-permute-done.5
  187.0 6.8 %fusion.30 = bf16[64,4096]{1,0:T(8,128)(2,1)} fusion(bf16[64,1024]{1,0:T(8,128)(2,1)S(1)} %bitcast_select_fusion, bf16[1,4096,1024]{2,1,0:T(8,128)(2,1)} %param.8), kind=kOutput, calls=%fused_computation.25 | convolution fusion | flops 537395200 | bytes 9043968 | tf_op jit(solution)/shard_map/dot_general | solution.py:67
  194.3 6.8 %multiply_convert_fusion = bf16[4096,1024]{1,0:T(8,128)(2,1)} fusion(bf16[64,4096]{1,0:T(8,128)(2,1)S(1)} %get-tuple-element.12, bf16[64,4096]{1,0:T(8,128)(2,1)} %get-tuple-element.10, bf16[64,4096]{1,0:T(8,128)(2,1)} %get-tuple-element.8, bf16[64,4096]{1,0:T(8,128)(2,1)S(1)} %get-tuple-element.6, bf16[64,1024]{1,0:T(8,128)(2,1)S(1)} %bitcast_select_fusion, ...), kind=kOutput, calls=%fused_computation | convolution fusion | flops 2166358016 | bytes 11010048 | tf_op jit(solution)/shard_map/dot_general | solution.py:89
  202.0 19.3 %all-gather = bf16[1,1,64,4096]{3,2,1,0:T(8,128)(2,1)S(1)} all-gather(bf16[1,1,64,1024]{3,2,1,0:T(8,128)(2,1)S(1)} %copy-done), channel_id=2, replica_groups=mesh['section'=4,'dp'=2,'tensor'=4] {'tensor'}, dimensions={3}, use_global_device_ids=true | all-gather | bytes 655360 | tf_op jit(solution)/shard_map/all_gather | solution.py:56
  221.5 5.1 %fusion.66 = bf16[64,1024]{1,0:T(8,128)(2,1)S(1)} fusion(bf16[1,4096,1024]{2,1,0:T(8,128)(2,1)} %param.8, bf16[1,1,64,4096]{3,2,1,0:T(8,128)(2,1)S(1)} %all-gather, f32[64]{0:T(128)S(1)} %add_rsqrt_fusion.7, bf16[1,1,64,1024]{3,2,1,0:T(8,128)(2,1)S(1)} %copy-done), kind=kOutput, calls=%fused_computation.59 | convolution fusion | flops 537919488 | bytes 9175296 | tf_op jit(solution)/shard_map/dot_general | solution.py:61
  226.6 3.1 collective-permute-start
  230.7 15.9 %all_gather.25 = bf16[64,4096]{1,0:T(8,128)(2,1)S(1)} all-gather(bf16[64,1024]{1,0:T(8,128)(2,1)S(1)} %bitcast_select_fusion.5), channel_id=1, replica_groups=mesh['section'=4,'dp'=2,'tensor'=4] {'tensor'}, dimensions={1}, use_global_device_ids=true | all-gather | bytes 655360 | tf_op jit(solution)/shard_map/all_gather | solution.py:56
  246.8 5.4 %add_convert_fusion.2 = bf16[64,1024]{1,0:T(8,128)(2,1)S(1)} fusion(bf16[64,1024]{1,0:T(8,128)(2,1)S(1)} %bitcast_select_fusion.5, bf16[1,4096,1024]{2,1,0:T(8,128)(2,1)} %param.8, bf16[64,4096]{1,0:T(8,128)(2,1)S(1)} %all_gather.25, f32[64]{0:T(128)S(1)} %add_rsqrt_fusion.6), kind=kOutput, calls=%fused_computation.112 | convolution fusion | flops 537919488 | bytes 9175296 | tf_op jit(solution)/shard_map/dot_general | solution.py:61
  252.3 2.1 collective-permute-start.1
  255.4 15.9 %all_gather.26 = bf16[64,4096]{1,0:T(8,128)(2,1)S(1)} all-gather(bf16[64,1024]{1,0:T(8,128)(2,1)S(1)} %bitcast_select_fusion.4), channel_id=1, replica_groups=mesh['section'=4,'dp'=2,'tensor'=4] {'tensor'}, dimensions={1}, use_global_device_ids=true | all-gather | bytes 655360 | tf_op jit(solution)/shard_map/all_gather | solution.py:56
  271.5 1.6 add_convert_fusion.1
  273.1 4.9 %collective-permute-start.2 = (bf16[64,1024]{1,0:T(8,128)(2,1)S(1)}, bf16[64,1024]{1,0:T(8,128)(2,1)S(1)}, u32[]{:S(2)}, u32[]{:S(2)}) collective-permute-start(bf16[64,1024]{1,0:T(8,128)(2,1)S(1)} %add_convert_fusion.1), channel_id=1, source_target_pairs={{0,8},{8,16},{16,24},{1,9},{9,17},{17,25},{2,10},{10,18},{18,26},{... | collective-permute-start | bytes 393224 | tf_op jit(solution)/shard_map/ppermute | solution.py:16
  279.0 16.2 %all_gather.27 = bf16[64,4096]{1,0:T(8,128)(2,1)S(1)} all-gather(bf16[64,1024]{1,0:T(8,128)(2,1)S(1)} %bitcast_select_fusion.3), channel_id=1, replica_groups=mesh['section'=4,'dp'=2,'tensor'=4] {'tensor'}, dimensions={1}, use_global_device_ids=true | all-gather | bytes 655360 | tf_op jit(solution)/shard_map/all_gather | solution.py:56
  295.5 1.7 fusion.113
  299.0 10.3 %psum.31 = f32[64,1]{0,1:T(1,128)S(1)} all-reduce(f32[64,1]{0,1:T(1,128)S(1)} %bitcast.159), channel_id=1, replica_groups=mesh['section'=4,'dp'=2,'tensor'=4] {'tensor'}, use_global_device_ids=true, to_apply=%region_19.20 | all-reduce | flops 64 | bytes 512 | tf_op jit(solution)/shard_map/psum | solution.py:79
  311.2 9.8 %reduce-scatter.14.cloned.1.call-done = bf16[2048,1024]{1,0:T(8,128)(2,1)} async-done(((bf16[4096,1024]{1,0:T(8,128)(2,1)}), bf16[2048,1024]{1,0:T(8,128)(2,1)}) %reduce-scatter.14.cloned.1.call-update) | async-done | bytes 4194320 | tf_op jit(solution)/shard_map/reduce_scatter | solution.py:94
  321.1 8.3 %fusion.42 = (bf16[1,2048,1024]{2,1,0:T(8,128)(2,1)}, bf16[1,2048,1024]{2,1,0:T(8,128)(2,1)}) fusion(bf16[2048,1024]{1,0:T(8,128)(2,1)} %reduce-scatter.14.cloned.1.call-done, bf16[1,2048,1024]{2,1,0:T(8,128)(2,1)} %param.10, bf16[1,2048,1024]{2,1,0:T(8,128)(2,1)} %param.9), kind=kLoop, calls=%fused_computation.29 | loop fusion | flops 18874368 | bytes 20971520 | tf_op jit(solution)/shard_map/broadcast_in_dim | solution.py:101
  (71 shorter events, 22.5 us)
Async XLA Ops:
  7.2 72.0 %copy-start.1 = (bf16[1,1,64,1024]{3,2,1,0:T(8,128)(2,1)S(1)}, bf16[1,1,64,1024]{3,2,1,0:T(8,128)(2,1)}, u32[]{:S(2)}) copy-start(bf16[1,1,64,1024]{3,2,1,0:T(8,128)(2,1)} %param.13) | copy-start | bytes 393220
  7.2 7.1 %copy-start.2 = (bf16[1,1,4,64,1024]{4,3,2,1,0:T(8,128)(2,1)S(1)}, bf16[1,1,4,64,1024]{4,3,2,1,0:T(8,128)(2,1)}, u32[]{:S(2)}) copy-start(bf16[1,1,4,64,1024]{4,3,2,1,0:T(8,128)(2,1)} %param.15) | copy-start | bytes 1572868
  7.2 62.0 %reduce-scatter.6.cloned.1.call-start = ((), (), s32[]{:S(2)}) async-start(), calls=%async_computation.5 | async-start | bytes 655360 | tf_op jit(solution)/shard_map/reduce_scatter | solution.py:76
  14.2 99.9 %reduce-scatter.8.cloned.1.call-start = ((), (), s32[]{:S(2)}) async-start(), calls=%async_computation.6 | async-start | bytes 655360 | tf_op jit(solution)/shard_map/reduce_scatter | solution.py:76
  80.2 3.2 collective-permute-start.3
  91.3 80.8 %reduce-scatter.10.cloned.1.call-start = ((), (), s32[]{:S(2)}) async-start(), calls=%async_computation.7 | async-start | bytes 655360 | tf_op jit(solution)/shard_map/reduce_scatter | solution.py:76
  124.9 17.2 %collective-permute-start.4 = (bf16[64,1024]{1,0:T(8,128)(2,1)S(1)}, bf16[64,1024]{1,0:T(8,128)(2,1)S(1)}, u32[]{:S(2)}, u32[]{:S(2)}) collective-permute-start(bf16[64,1024]{1,0:T(8,128)(2,1)S(1)} %fusion.104), channel_id=1, source_target_pairs={{8,0},{16,8},{24,16},{9,1},{17,9},{25,17},{10,2},{18,10},{26,18},{... | collective-permute-start | bytes 393224 | tf_op jit(solution)/shard_map/ppermute | solution.py:16
  149.8 148.2 %reduce-scatter.12.cloned.1.call-start = ((), (), s32[]{:S(2)}) async-start(), calls=%async_computation.8 | async-start | bytes 655360 | tf_op jit(solution)/shard_map/reduce_scatter | solution.py:76
  182.8 3.2 collective-permute-start.5
  193.8 127.2 %reduce-scatter.14.cloned.1.call-start = ((), (), s32[]{:S(2)}) async-start(), calls=%async_computation.9 | async-start | bytes 12582912 | tf_op jit(solution)/shard_map/reduce_scatter | solution.py:94
  201.1 0.9 copy-start
  221.5 9.2 %copy-start.3 = (bf16[1,3,64,1024]{3,2,1,0:T(8,128)(2,1)S(1)}, bf16[1,3,64,1024]{3,2,1,0:T(8,128)(2,1)}, u32[]{:S(2)}) copy-start(bf16[1,3,64,1024]{3,2,1,0:T(8,128)(2,1)} %param.12) | copy-start | bytes 1179652
  226.6 4.1 %collective-permute-start = (bf16[64,1024]{1,0:T(8,128)(2,1)S(1)}, bf16[64,1024]{1,0:T(8,128)(2,1)S(1)}, u32[]{:S(2)}, u32[]{:S(2)}) collective-permute-start(bf16[64,1024]{1,0:T(8,128)(2,1)S(1)} %fusion.66), channel_id=1, source_target_pairs={{0,8},{8,16},{16,24},{1,9},{9,17},{17,25},{2,10},{10,18},{18,26},{... | collective-permute-start | bytes 393224 | tf_op jit(solution)/shard_map/ppermute | solution.py:16
  230.7 40.8 %slice-start = ((s8[8388608]{0:T(1024)(128)(4,1)}), s8[4194304]{0:T(1024)(128)(4,1)S(1)}, s32[]{:S(2)}) async-start(s8[8388608]{0:T(1024)(128)(4,1)} %bitcast.147), calls=%async_computation.10 | async-start | bytes 8388608
  246.8 24.6 %slice-start.1 = ((s8[8388608]{0:T(1024)(128)(4,1)}), s8[4194304]{0:T(1024)(128)(4,1)S(1)}, s32[]{:S(2)}) async-start(s8[8388608]{0:T(1024)(128)(4,1)} %bitcast.147), calls=%async_computation.11 | async-start | bytes 8388608
  252.3 3.1 collective-permute-start.1
  273.1 5.9 %collective-permute-start.2 = (bf16[64,1024]{1,0:T(8,128)(2,1)S(1)}, bf16[64,1024]{1,0:T(8,128)(2,1)S(1)}, u32[]{:S(2)}, u32[]{:S(2)}) collective-permute-start(bf16[64,1024]{1,0:T(8,128)(2,1)S(1)} %add_convert_fusion.1), channel_id=1, source_target_pairs={{0,8},{8,16},{16,24},{1,9},{9,17},{17,25},{2,10},{10,18},{18,26},{... | collective-permute-start | bytes 393224 | tf_op jit(solution)/shard_map/ppermute | solution.py:16
Sparse Core Ops, SparseCore 0:
  14.4 27.4 reduce-scatter.5
  91.4 22.7 reduce-scatter.7
  149.9 22.1 reduce-scatter.9
  194.0 25.5 reduce-scatter.11
  221.7 99.3 reduce-scatter.13
where the time goes:
time: 337 us; the launch traced here: 336 us
  blocking collectives  174 us (52%)
  waiting for transfers between devices  59.4 us (18%)
  matrix products  48.1 us (14%)
  other arithmetic  25.3 us (8%)
  starting transfers between devices  14.4 us (4%)
  between operations  14 us (4%)
    all_gather x4, blocking collectives, body(): lax.all_gather(stashed[0, 0, tick_index], 'tensor', axis=1, tiled=True)  70.1 us
    all_gather x4, blocking collectives, body(): lax.all_gather(current_input, 'tensor', axis=1, tiled=True)  67.3 us
    reduce_scatter x4, waiting for transfers between devices, body(): lax.psum_scatter(partial_value, 'tensor', scatter_dimension=1, tiled=True)  42.9 us
    psum x4, blocking collectives, body(): lax.psum(jnp.sum(own_grad * own_hat, axis=-1, keepdims=True), 'tensor')  36.5 us
    dot_general x4, matrix products, body(): lax.dot_general(current_gradient, weight, (((1,), (1,)), ((), ())), prefe...  27.5 us
    ppermute x6, starting transfers between devices, shifted(): return lax.ppermute(block, axis, route)  14 us
    dot_general x4, matrix products, body(): jnp.dot(x_hat.astype(jnp.bfloat16), weight, preferred_element_type=jnp.fl...  13.8 us
    reduce_scatter x1, waiting for transfers between devices, body(): lax.psum_scatter(replica_term, 'dp', scatter_dimension=0, tiled=True)  9.84 us
  transfers between devices with their start and end apart: 11, of which 8 were waited for; matrix products, arithmetic and copies ran while one was open for 9% of the time, Pallas kernels for 0%

commit v1 on v0

v1 whole, which is shorter than its diff:
```python
import functools
import math

import jax
import jax.numpy as jnp
from jax import lax
from jax.experimental import pallas as pl
from jax.experimental.pallas import tpu as pltpu
from jax.sharding import PartitionSpec as P

EPSILON = 1e-06
MOMENTUM_RATE = 0.9
LEARNING_RATE = 0.05
MESH = pl.DeviceIdType.MESH
LANES = 128


def remote(src, dst, send_sem, recv_sem, target):
    return pltpu.make_async_remote_copy(
        src_ref=src,
        dst_ref=dst,
        send_sem=send_sem,
        recv_sem=recv_sem,
        device_id=target,
        device_id_type=MESH,
    )


def rowsum(values):
    return jnp.sum(values, axis=-1, keepdims=True)


def window_kernel(
    n, dp, sections,
    w_hbm, x0_hbm, inc_hbm, g0_hbm, loss_hbm, stash_hbm,
    fwd, bwd, st_all, sg_all,
    w, xg, st, gbuf, prod, acc, ssq, stw, ksc, sgs,
    rs_s, rs_r, inm, inb,
    lsem, x_ss, x_rs, st_ss, st_rs, rs_ss, rs_rs,
    f_ss, f_rs, b_ss, b_rs, in_ss, in_rs,
    dst_ss, dst_rs, dsg_ss, dsg_rs, own_sem,
):
    j = lax.axis_index("tensor")
    d = lax.axis_index("dp")
    s = lax.axis_index("section")
    ticks, _, rows, cols = xg.shape
    extent = n * cols
    root = math.sqrt(extent)
    nb = n // dp
    first, last = s == 0, s == sections - 1

    def both(a, b):
        return jnp.logical_and(a, b)

    w_copy = pltpu.make_async_copy(w_hbm, w, lsem.at[0])
    st_copy = pltpu.make_async_copy(stash_hbm, st.at[:, j], lsem.at[1])
    x_copy = pltpu.make_async_copy(x0_hbm, xg.at[0, j], lsem.at[2])
    g_copy = pltpu.make_async_copy(g0_hbm, gbuf.at[0], lsem.at[3])
    inc_copy = pltpu.make_async_copy(inc_hbm, xg.at[pl.ds(1, ticks - 1), j], lsem.at[4])
    loss_copy = pltpu.make_async_copy(loss_hbm, gbuf.at[pl.ds(1, ticks - 1)], lsem.at[5])
    st_copy.start()
    x_copy.start()
    g_copy.start()
    pl.when(first)(lambda: inc_copy.start())
    pl.when(last)(lambda: loss_copy.start())
    w_copy.start()

    barrier = pltpu.get_barrier_semaphore()
    for q in range(1, n):
        pl.semaphore_signal(
            barrier, inc=1, device_id={"tensor": lax.rem(j + q, n)}, device_id_type=MESH
        )
    for q in range(1, dp):
        pl.semaphore_signal(
            barrier, inc=1, device_id={"dp": lax.rem(d + q, dp)}, device_id_type=MESH
        )

    @pl.when(s > 0)
    def _():
        pl.semaphore_signal(barrier, inc=1, device_id={"section": s - 1}, device_id_type=MESH)

    @pl.when(s < sections - 1)
    def _():
        pl.semaphore_signal(barrier, inc=1, device_id={"section": s + 1}, device_id_type=MESH)

    peers = n - 1 + dp - 1 + jnp.where(s > 0, 1, 0) + jnp.where(s < sections - 1, 1, 0)
    pl.semaphore_wait(barrier, peers)
    st_copy.wait()
    x_copy.wait()
    g_copy.wait()
    pl.when(first)(lambda: inc_copy.wait())
    pl.when(last)(lambda: loss_copy.wait())

    def line_copy(buf, ss, rs, t, side, k, block):
        return remote(
            buf.at[t, block], buf.at[t, block], ss.at[t, side, k], rs.at[t, side, k],
            {"tensor": j + 1 if side == 0 else j - 1},
        )

    def send_ok(side, k):
        if side == 0:
            return both(j < n - 1, j - k >= 0)
        return both(j > 0, j + k <= n - 1)

    def line_send(buf, ss, rs, t, side, k, extra=None):
        if k > n - 2:
            return
        ok = send_ok(side, k)
        ok = ok if extra is None else both(ok, extra)

        @pl.when(ok)
        def _():
            line_copy(buf, ss, rs, t, side, k, j - k if side == 0 else j + k).start()

    def line_sent(buf, ss, rs, t, side, k):
        @pl.when(send_ok(side, k))
        def _():
            line_copy(buf, ss, rs, t, side, k, j - k if side == 0 else j + k).wait_send()

    def arrives(side, k):
        return j - 1 - k >= 0 if side == 0 else j + 1 + k <= n - 1

    def line_recv(buf, ss, rs, t, side, k, extra=None):
        ok = arrives(side, k)
        ok = ok if extra is None else both(ok, extra)
        block = j - 1 - k if side == 0 else j + 1 + k

        @pl.when(ok)
        def _():
            remote(
                buf.at[t, block], buf.at[t, block], ss.at[t, side, k], rs.at[t, side, k],
                {"tensor": j - 1 if side == 0 else j + 1},
            ).wait_recv()

    xs = (xg, x_ss, x_rs)
    sts = (st, st_ss, st_rs)

    def dp_stash(t, q, i):
        peer = lax.rem(d + q, dp)
        return remote(
            st.at[t, peer * nb + i], st_all.at[i, d, t],
            dst_ss.at[t, q - 1, i], dst_rs.at[t, q - 1, i], {"dp": peer},
        )

    def dp_stash_in(t, q, i):
        peer = lax.rem(d + dp - q, dp)
        return remote(
            st.at[t, i], st_all.at[i, peer, t],
            dst_ss.at[t, q - 1, i], dst_rs.at[t, q - 1, i], {"dp": peer},
        )

    def dp_grad(t, q):
        peer = lax.rem(d + q, dp)
        return remote(
            sgs.at[t], sg_all.at[d, t], dsg_ss.at[t, q - 1], dsg_rs.at[t, q - 1], {"dp": peer}
        )

    def dp_grad_in(t, q):
        peer = lax.rem(d + dp - q, dp)
        return remote(
            sgs.at[t], sg_all.at[peer, t], dsg_ss.at[t, q - 1], dsg_rs.at[t, q - 1], {"dp": peer}
        )

    def own_stash(t, i):
        return pltpu.make_async_copy(st.at[t, d * nb + i], st_all.at[i, d, t], own_sem.at[t, i])

    def own_grad_copy(t):
        return pltpu.make_async_copy(sgs.at[t], sg_all.at[d, t], own_sem.at[t, nb])

    def stash_finish(t):
        for q in range(1, dp):
            for i in range(nb):
                dp_stash(t, q, i).start()
        for i in range(nb):
            own_stash(t, i).start()
        stw[...] = jnp.zeros_like(stw)

        def one(b, total):
            block = st[t, b]
            stw[...] += jnp.dot(block, w[b], preferred_element_type=jnp.float32)
            wide = block.astype(jnp.float32)
            return total + rowsum(wide * wide)

        total = lax.fori_loop(0, n, one, jnp.zeros((rows, 1), jnp.float32))
        ksc[...] = jnp.broadcast_to(lax.rsqrt(total / extent + EPSILON), ksc.shape)

    def rs_copy(t, side, k):
        return remote(
            rs_s.at[t, side, k], rs_r.at[t, side, k], rs_ss.at[t, side, k], rs_rs.at[t, side, k],
            {"tensor": j + 1 if side == 0 else j - 1},
        )

    def rs_in(t, side, k):
        return remote(
            rs_s.at[t, side, 0], rs_r.at[t, side, k], rs_ss.at[t, side, 0], rs_rs.at[t, side, k],
            {"tensor": j - 1 if side == 0 else j + 1},
        )

    def inner_copy(t, q):
        return remote(
            inm.at[t], inb.at[t, q - 1], in_ss.at[t, q - 1], in_rs.at[t, q - 1],
            {"tensor": lax.rem(j + q, n)},
        )

    def inner_in(t, q):
        return remote(
            inm.at[t], inb.at[t, q - 1], in_ss.at[t, q - 1], in_rs.at[t, q - 1],
            {"tensor": lax.rem(j + n - q, n)},
        )

    def fwd_copy(t):
        return remote(
            fwd.at[t], xg.at[t + 1, j], f_ss.at[t + 1], f_rs.at[t + 1], {"section": s + 1}
        )

    def bwd_copy(t):
        return remote(
            bwd.at[t], gbuf.at[t + 1], b_ss.at[t + 1], b_rs.at[t + 1], {"section": s - 1}
        )

    order = []
    for k in range((n + 1) // 2):
        order += [n - 1 - k] + ([k] if k != n - 1 - k else [])

    for side in range(2):
        line_send(*sts, 0, side, 0)
    for k in range(n - 1):
        for side in range(2):
            line_recv(*sts, 0, side, k)
            line_send(*sts, 0, side, k + 1)
    w_copy.wait()
    stash_finish(0)

    def tick(t, carry):
        more = t < ticks - 1

        @pl.when(both(t > 0, s > 0))
        def _():
            remote(
                fwd.at[t], xg.at[t, j], f_ss.at[t], f_rs.at[t], {"section": s - 1}
            ).wait_recv()

        for side in range(2):
            line_send(*xs, t, side, 0)

        @pl.when(both(t > 0, s < sections - 1))
        def _():
            remote(
                bwd.at[t], gbuf.at[t], b_ss.at[t], b_rs.at[t], {"section": s + 1}
            ).wait_recv()

        wide = gbuf[t].astype(jnp.float32)
        products = wide * stw[...]
        part = products[:, :LANES]
        for i in range(1, cols // LANES):
            part = part + products[:, i * LANES:(i + 1) * LANES]
        inm[t] = part
        sgs[t] = (wide * (ksc[:, :1] * (1.0 / root))).astype(jnp.bfloat16)
        for q in range(1, n):
            inner_copy(t, q).start()
        for q in range(1, dp):
            dp_grad(t, q).start()
        own_grad_copy(t).start()

        for b in order:
            prod[b] = lax.dot_general(
                gbuf[t], w[b], (((1,), (1,)), ((), ())), preferred_element_type=jnp.float32
            )
            if b >= 1:
                @pl.when(j == 0)
                def _():
                    rs_s[t, 0, n - 1 - b] = prod[b].astype(jnp.bfloat16)
                    rs_copy(t, 0, n - 1 - b).start()
            if b <= n - 2:
                @pl.when(j == n - 1)
                def _():
                    rs_s[t, 1, b] = prod[b].astype(jnp.bfloat16)
                    rs_copy(t, 1, b).start()

        def take(block):
            value = xg[t, block]
            acc[...] += jnp.dot(value, w[block], preferred_element_type=jnp.float32)
            value_wide = value.astype(jnp.float32)
            ssq[...] += jnp.broadcast_to(rowsum(value_wide * value_wide), ssq.shape)

        acc[...] = jnp.zeros_like(acc)
        ssq[...] = jnp.zeros_like(ssq)
        take(j)

        for k in range(n - 1):
            for side in range(2):
                line_recv(*xs, t, side, k)
                line_send(*xs, t, side, k + 1)
            for side in range(2):
                if k > 0:
                    line_recv(*sts, t + 1, side, k - 1, more)
                line_send(*sts, t + 1, side, k, more)

            up, down = n - 1 - k, k

            @pl.when(both(j > 0, j < up))
            def _():
                rs_in(t, 0, k).wait_recv()
                rs_s[t, 0, k] = (prod[up] + rs_r[t, 0, k].astype(jnp.float32)).astype(jnp.bfloat16)
                rs_copy(t, 0, k).start()

            @pl.when(both(j < n - 1, j > down))
            def _():
                rs_in(t, 1, k).wait_recv()
                rs_s[t, 1, k] = (prod[down] + rs_r[t, 1, k].astype(jnp.float32)).astype(jnp.bfloat16)
                rs_copy(t, 1, k).start()

            for side in range(2):
                block = j - 1 - k if side == 0 else j + 1 + k
                pl.when(arrives(side, k))(lambda block=block: take(block))

        factor = lax.rsqrt(ssq[:, :1] / extent + EPSILON) * (1.0 / root)
        fwd[t] = (xg[t, j].astype(jnp.float32) + acc[...] * factor).astype(jnp.bfloat16)
        pl.when(both(more, s < sections - 1))(lambda: fwd_copy(t).start())

        @pl.when(j > 0)
        def _():
            rs_in(t, 0, n - 1 - j).wait_recv()
            prod[j] += rs_r[t, 0, n - 1 - j].astype(jnp.float32)

        @pl.when(j < n - 1)
        def _():
            rs_in(t, 1, j).wait_recv()
            prod[j] += rs_r[t, 1, j].astype(jnp.float32)

        inner = inm[t]
        for q in range(1, n):
            inner_in(t, q).wait_recv()
            inner = inner + inb[t, q - 1]
        scale = ksc[:, :1]
        inner_dot = rowsum(inner) * scale * (1.0 / (root * extent))
        kept = st[t, j].astype(jnp.float32) * scale
        bwd[t] = (
            gbuf[t].astype(jnp.float32)
            + scale * (prod[j] * (1.0 / root) - kept * inner_dot)
        ).astype(jnp.bfloat16)
        pl.when(both(more, s > 0))(lambda: bwd_copy(t).start())

        for side in range(2):
            line_recv(*sts, t + 1, side, n - 2, more)
        pl.when(more)(lambda: stash_finish(t + 1))
        return carry

    lax.fori_loop(0, ticks, tick, 0)

    def drain(t, carry):
        for q in range(1, dp):
            for i in range(nb):
                dp_stash(t, q, i).wait_send()
                dp_stash_in(t, q, i).wait_recv()
            dp_grad(t, q).wait_send()
            dp_grad_in(t, q).wait_recv()
        for i in range(nb):
            own_stash(t, i).wait()
        own_grad_copy(t).wait()
        for q in range(1, n):
            inner_copy(t, q).wait_send()
        for k in range(n - 1):
            for side in range(2):
                line_sent(*xs, t, side, k)
                line_sent(*sts, t, side, k)
            pl.when(j < n - 1 - k)(lambda: rs_copy(t, 0, k).wait_send())
            pl.when(j > k)(lambda: rs_copy(t, 1, k).wait_send())
        pl.when(both(t < ticks - 1, s < sections - 1))(lambda: fwd_copy(t).wait_send())
        pl.when(both(t < ticks - 1, s > 0))(lambda: bwd_copy(t).wait_send())
        return carry

    lax.fori_loop(0, ticks, drain, 0)


def update_kernel(st, sg, m, wn, w_out, m_out):
    grads = lax.dot_general(
        st[0], sg[...], (((0,), (0,)), ((), ())), preferred_element_type=jnp.float32
    )
    velocity = MOMENTUM_RATE * m[...].astype(jnp.float32) + grads
    w_out[...] = (wn[...].astype(jnp.float32) - LEARNING_RATE * velocity).astype(jnp.bfloat16)
    m_out[...] = velocity.astype(jnp.bfloat16)


def body(
    n, dp, sections,
    shadow_weight_copy, newest_weight_version, momentum, pending_section_input,
    incoming_micro_input, pending_output_gradient, loss_gradient_rows, stashed,
):
    extent, cols = shadow_weight_copy.shape[1:]
    ticks, rows = stashed.shape[2:4]
    nb = n // dp
    bf16, f32 = jnp.bfloat16, jnp.float32
    dma = pltpu.SemaphoreType.DMA
    anywhere = pl.BlockSpec(memory_space=pl.ANY)
    vmem = pl.BlockSpec(memory_space=pltpu.VMEM)
    fwd, bwd, st_all, sg_all = pl.pallas_call(
        functools.partial(window_kernel, n, dp, sections),
        out_shape=(
            jax.ShapeDtypeStruct((ticks, rows, cols), bf16),
            jax.ShapeDtypeStruct((ticks, rows, cols), bf16),
            jax.ShapeDtypeStruct((nb, dp, ticks, rows, cols), bf16),
            jax.ShapeDtypeStruct((dp, ticks, rows, cols), bf16),
        ),
        in_specs=[anywhere] * 6,
        out_specs=(vmem, vmem, anywhere, anywhere),
        scratch_shapes=[
            pltpu.VMEM((n, cols, cols), bf16),
            pltpu.VMEM((ticks, n, rows, cols), bf16),
            pltpu.VMEM((ticks, n, rows, cols), bf16),
            pltpu.VMEM((ticks, rows, cols), bf16),
            pltpu.VMEM((n, rows, cols), f32),
            pltpu.VMEM((rows, cols), f32),
            pltpu.VMEM((rows, LANES), f32),
            pltpu.VMEM((rows, cols), f32),
            pltpu.VMEM((rows, LANES), f32),
            pltpu.VMEM((ticks, rows, cols), bf16),
            pltpu.VMEM((ticks, 2, n - 1, rows, cols), bf16),
            pltpu.VMEM((ticks, 2, n - 1, rows, cols), bf16),
            pltpu.VMEM((ticks, rows, LANES), f32),
            pltpu.VMEM((ticks, n - 1, rows, LANES), f32),
            dma((6,)),
            dma((ticks, 2, n - 1)),
            dma((ticks, 2, n - 1)),
            dma((ticks, 2, n - 1)),
            dma((ticks, 2, n - 1)),
            dma((ticks, 2, n - 1)),
            dma((ticks, 2, n - 1)),
            dma((ticks,)),
            dma((ticks,)),
            dma((ticks,)),
            dma((ticks,)),
            dma((ticks, n - 1)),
            dma((ticks, n - 1)),
            dma((ticks, dp - 1, nb)),
            dma((ticks, dp - 1, nb)),
            dma((ticks, dp - 1)),
            dma((ticks, dp - 1)),
            dma((ticks, nb + 1)),
        ],
        compiler_params=pltpu.CompilerParams(
            collective_id=0, has_side_effects=True, vmem_limit_bytes=48 * 1024 * 1024
        ),
        name="window",
    )(
        shadow_weight_copy.reshape(n, cols, cols),
        pending_section_input[0, 0],
        incoming_micro_input[0],
        pending_output_gradient[0, 0],
        loss_gradient_rows[0],
        stashed[0, 0],
    )
    depth = dp * ticks * rows
    own_rows = extent // dp
    tile = min(256, cols)
    per_block = cols // tile
    wide = pl.BlockSpec((tile, cols), lambda i: (i, 0))
    w_next, m_next = pl.pallas_call(
        update_kernel,
        out_shape=(jax.ShapeDtypeStruct((own_rows, cols), bf16),) * 2,
        grid=(own_rows // tile,),
        in_specs=[
            pl.BlockSpec((1, depth, tile), lambda i: (i // per_block, 0, i % per_block)),
            pl.BlockSpec((depth, cols), lambda i: (0, 0)),
            wide,
            wide,
        ],
        out_specs=(wide, wide),
        name="update",
    )(
        st_all.reshape(nb, depth, cols),
        sg_all.reshape(depth, cols),
        momentum[0],
        newest_weight_version[0],
    )
    return (fwd[None, None], bwd[None, None], w_next[None], m_next[None])


def solution(mesh):
    return jax.shard_map(
        functools.partial(body, mesh.shape["tensor"], mesh.shape["dp"], mesh.shape["section"]),
        mesh=mesh,
        in_specs=(
            P("section", None, "tensor"),
            P("section", "dp", "tensor"),
            P("section", "dp", "tensor"),
            P("dp", "section", None, "tensor"),
            P("dp", None, None, "tensor"),
            P("dp", "section", None, "tensor"),
            P("dp", None, None, "tensor"),
            P("dp", "section", None, None, "tensor"),
        ),
        out_specs=(
            P("dp", "section", None, None, "tensor"),
            P("dp", "section", None, None, "tensor"),
            P("section", "dp", "tensor"),
            P("section", "dp", "tensor"),
        ),
        check_vma=False,
    )
```

time: 337 us -> 167 us (0.50)
  blocking collectives: 174 us -> 0 us
  Pallas kernels: 0 us -> 157 us
  waiting for transfers between devices: 59.4 us -> 0 us
  matrix products: 48.1 us -> 0 us
  other arithmetic: 25.3 us -> 0 us
  starting transfers between devices: 14.4 us -> 0 us
  between operations: 14 us -> 0.66 us
  local copies, waits for them, and re-layouts: 0.94 us -> 8.74 us
    pallas_call x0 -> x2, Pallas kernels: none -> 157 us  [the longest x1 145 us: body(): pl.pallas_call(functools.partial(window_kernel, n, dp, sections), out_sha...]
    all_gather x8 -> x0, blocking collectives: 137 us -> none  [the longest x4 70.1 us: body(): lax.all_gather(stashed[0, 0, tick_index], 'tensor', axis=1, tiled=True)]
    reduce_scatter x5 -> x0, waiting for transfers between devices: 52.7 us -> none  [the longest x4 42.9 us: body(): lax.psum_scatter(partial_value, 'tensor', scatter_dimension=1, tiled=True)]
    dot_general x9 -> x0, matrix products: 48.1 us -> none  [the longest x4 27.5 us: body(): lax.dot_general(current_gradient, weight, (((1,), (1,)), ((), ())), prefe...]
    psum x4 -> x0, blocking collectives: 36.5 us -> none  [body(): lax.psum(jnp.sum(own_grad * own_hat, axis=-1, keepdims=True), 'tensor')]
    ppermute x6 -> x0, starting transfers between devices: 14 us -> none  [shifted(): return lax.ppermute(block, axis, route)]
    broadcast_in_dim x3 -> x0, other arithmetic: 10.1 us -> none  [the longest x1 8.35 us: body(): m_next = velocity.astype(jnp.bfloat16)[None]]
    unnamed x12 -> x16, local copies, waits for them, and re-layouts: 0.9 us -> 8.74 us
  transfers between devices with their start and end apart: 11 -> 0, of which waited for: 8 -> 0; matrix products, arithmetic and copies ran while one was open for 9% -> 0% of each run, Pallas kernels for 0% -> 0%
where the time goes in v1:
time: 167 us; the launch traced here: 166 us
  Pallas kernels  157 us (94%)
  local copies, waits for them, and re-layouts  8.74 us (5%)
    pallas_call x1, Pallas kernels, body(): pl.pallas_call(functools.partial(window_kernel, n, dp, sections), out_sha...  145 us
    pallas_call x1, Pallas kernels, body(): pl.pallas_call(update_kernel, out_shape=(jax.ShapeDtypeStruct((own_rows,...  11.4 us
    unnamed x16, local copies, waits for them, and re-layouts  8.74 us

profile of v1, /device:TPU:0, one launch (start us, length us, event | category | flops | bytes accessed | tf_op | source)
XLA Modules:
  0.0 166.2 jit_solution(9261260250130464839)
XLA Ops:
  0.6 0.0 copy-start.2
  0.6 1.0 copy-done.2
  1.7 0.0 copy-start.3
  1.7 1.0 copy-done.3
  2.7 0.0 copy-start.4
  2.7 1.0 copy-done.4
  3.7 0.0 copy-start.5
  3.7 0.9 copy-done.5
  4.6 0.0 copy-start.6
  4.6 0.9 copy-done.6
  5.5 145.4 %window.1 = (bf16[4,64,1024]{2,1,0:T(8,128)(2,1)S(1)}, bf16[4,64,1024]{2,1,0:T(8,128)(2,1)S(1)}, bf16[2,2,4,64,1024]{4,3,2,1,0:T(8,128)(2,1)S(1)}, bf16[2,4,64,1024]{3,2,1,0:T(8,128)(2,1)S(1)}) custom-call(bf16[4,1024,1024]{2,1,0:T(8,128)(2,1)} %bitcast.23, bf16[64,1024]{1,0:T(8,128)(2,1)S(1)} %bitcast.21, bf16[3,64,1024]{2,1,0:T(8,128)(2,1)S(1)} %bitcast.19, ...), custom_call_target="tpu_custom_call" | custom-call | tf_op jit(solution)/shard_map/window/pallas_call | solution.py:397
  150.9 0.0 copy-start
  150.9 1.3 copy-done
  152.2 0.0 copy-start.1
  152.3 1.0 copy-done.1
  153.2 11.4 %update.1 = (bf16[2048,1024]{1,0:T(8,128)(2,1)}, bf16[2048,1024]{1,0:T(8,128)(2,1)}) custom-call(bf16[2,512,1024]{2,1,0:T(8,128)(2,1)} %bitcast.14, bf16[512,1024]{1,0:T(8,128)(2,1)} %bitcast.15, bf16[2048,1024]{1,0:T(8,128)(2,1)} %bitcast.24, bf16[2048,1024]{1,0:T(8,128)(2,1)} %bitcast.25), custom_call_target="tpu_custom_call" | custom-call | tf_op jit(solution)/shard_map/update/pallas_call | solution.py:458
  164.7 0.8 copy.14
  165.4 0.8 copy.15
Async XLA Ops:
  0.6 1.0 copy-start.2
  1.7 1.0 copy-start.3
  2.7 1.0 copy-start.4
  3.7 0.9 copy-start.5
  4.6 0.9 copy-start.6
  150.9 1.3 copy-start
  152.2 1.0 copy-start.1

commit v2 on v1

--- a/solution.py
+++ b/solution.py
@@ -47,6 +47,8 @@
     extent = n * cols
     root = math.sqrt(extent)
     nb = n // dp
+    half = rows // 2
+    halves = [pl.ds(h * half, half) for h in range(2)]
     first, last = s == 0, s == sections - 1
 
     def both(a, b):
@@ -91,9 +93,10 @@
     pl.when(first)(lambda: inc_copy.wait())
     pl.when(last)(lambda: loss_copy.wait())
 
-    def line_copy(buf, ss, rs, t, side, k, block):
-        return remote(
-            buf.at[t, block], buf.at[t, block], ss.at[t, side, k], rs.at[t, side, k],
+    def line_copy(buf, ss, rs, t, side, k, h, block):
+        piece = buf.at[t, block, halves[h]]
+        return remote(
+            piece, piece, ss.at[t, side, k, h], rs.at[t, side, k, h],
             {"tensor": j + 1 if side == 0 else j - 1},
         )
 
@@ -102,7 +105,7 @@
             return both(j < n - 1, j - k >= 0)
         return both(j > 0, j + k <= n - 1)
 
-    def line_send(buf, ss, rs, t, side, k, extra=None):
+    def line_send(buf, ss, rs, t, side, k, h, extra=None):
         if k > n - 2:
             return
         ok = send_ok(side, k)
@@ -110,25 +113,26 @@
 
         @pl.when(ok)
         def _():
-            line_copy(buf, ss, rs, t, side, k, j - k if side == 0 else j + k).start()
-
-    def line_sent(buf, ss, rs, t, side, k):
+            line_copy(buf, ss, rs, t, side, k, h, j - k if side == 0 else j + k).start()
+
+    def line_sent(buf, ss, rs, t, side, k, h):
         @pl.when(send_ok(side, k))
         def _():
-            line_copy(buf, ss, rs, t, side, k, j - k if side == 0 else j + k).wait_send()
+            line_copy(buf, ss, rs, t, side, k, h, j - k if side == 0 else j + k).wait_send()
 
     def arrives(side, k):
         return j - 1 - k >= 0 if side == 0 else j + 1 + k <= n - 1
 
-    def line_recv(buf, ss, rs, t, side, k, extra=None):
+    def line_recv(buf, ss, rs, t, side, k, h, extra=None):
         ok = arrives(side, k)
         ok = ok if extra is None else both(ok, extra)
         block = j - 1 - k if side == 0 else j + 1 + k
 
         @pl.when(ok)
         def _():
+            piece = buf.at[t, block, halves[h]]
             remote(
-                buf.at[t, block], buf.at[t, block], ss.at[t, side, k], rs.at[t, side, k],
+                piece, piece, ss.at[t, side, k, h], rs.at[t, side, k, h],
                 {"tensor": j - 1 if side == 0 else j + 1},
             ).wait_recv()
 
@@ -184,15 +188,17 @@
         total = lax.fori_loop(0, n, one, jnp.zeros((rows, 1), jnp.float32))
         ksc[...] = jnp.broadcast_to(lax.rsqrt(total / extent + EPSILON), ksc.shape)
 
-    def rs_copy(t, side, k):
-        return remote(
-            rs_s.at[t, side, k], rs_r.at[t, side, k], rs_ss.at[t, side, k], rs_rs.at[t, side, k],
+    def rs_copy(t, side, k, h):
+        return remote(
+            rs_s.at[t, side, k, halves[h]], rs_r.at[t, side, k, halves[h]],
+            rs_ss.at[t, side, k, h], rs_rs.at[t, side, k, h],
             {"tensor": j + 1 if side == 0 else j - 1},
         )
 
-    def rs_in(t, side, k):
-        return remote(
-            rs_s.at[t, side, 0], rs_r.at[t, side, k], rs_ss.at[t, side, 0], rs_rs.at[t, side, k],
+    def rs_in(t, side, k, h):
+        return remote(
+            rs_s.at[t, side, 0, halves[h]], rs_r.at[t, side, k, halves[h]],
+            rs_ss.at[t, side, 0, h], rs_rs.at[t, side, k, h],
             {"tensor": j - 1 if side == 0 else j + 1},
         )
 
@@ -222,12 +228,14 @@
     for k in range((n + 1) // 2):
         order += [n - 1 - k] + ([k] if k != n - 1 - k else [])
 
-    for side in range(2):
-        line_send(*sts, 0, side, 0)
+    for h in range(2):
+        for side in range(2):
+            line_send(*sts, 0, side, 0, h)
     for k in range(n - 1):
-        for side in range(2):
-            line_recv(*sts, 0, side, k)
-            line_send(*sts, 0, side, k + 1)
+        for h in range(2):
+            for side in range(2):
+                line_recv(*sts, 0, side, k, h)
+                line_send(*sts, 0, side, k + 1, h)
     w_copy.wait()
     stash_finish(0)
 
@@ -240,8 +248,9 @@
                 fwd.at[t], xg.at[t, j], f_ss.at[t], f_rs.at[t], {"section": s - 1}
             ).wait_recv()
 
-        for side in range(2):
-            line_send(*xs, t, side, 0)
+        for h in range(2):
+            for side in range(2):
+                line_send(*xs, t, side, 0, h)
 
         @pl.when(both(t > 0, s < sections - 1))
         def _():
@@ -270,12 +279,14 @@
                 @pl.when(j == 0)
                 def _():
                     rs_s[t, 0, n - 1 - b] = prod[b].astype(jnp.bfloat16)
-                    rs_copy(t, 0, n - 1 - b).start()
+                    for h in range(2):
+                        rs_copy(t, 0, n - 1 - b, h).start()
             if b <= n - 2:
                 @pl.when(j == n - 1)
                 def _():
                     rs_s[t, 1, b] = prod[b].astype(jnp.bfloat16)
-                    rs_copy(t, 1, b).start()
+                    for h in range(2):
+                        rs_copy(t, 1, b, h).start()
 
         def take(block):
             value = xg[t, block]
@@ -288,31 +299,39 @@
         take(j)
 
         for k in range(n - 1):
-            for side in range(2):
-                line_recv(*xs, t, side, k)
-                line_send(*xs, t, side, k + 1)
-            for side in range(2):
-                if k > 0:
-                    line_recv(*sts, t + 1, side, k - 1, more)
-                line_send(*sts, t + 1, side, k, more)
+            for h in range(2):
+                for side in range(2):
+                    line_recv(*xs, t, side, k, h)
+                    line_send(*xs, t, side, k + 1, h)
 
             up, down = n - 1 - k, k
 
             @pl.when(both(j > 0, j < up))
             def _():
-                rs_in(t, 0, k).wait_recv()
-                rs_s[t, 0, k] = (prod[up] + rs_r[t, 0, k].astype(jnp.float32)).astype(jnp.bfloat16)
-                rs_copy(t, 0, k).start()
+                for h in range(2):
+                    at = halves[h]
+                    rs_in(t, 0, k, h).wait_recv()
+                    total = prod[up, at] + rs_r[t, 0, k, at].astype(jnp.float32)
+                    rs_s[t, 0, k, at] = total.astype(jnp.bfloat16)
+                    rs_copy(t, 0, k, h).start()
 
             @pl.when(both(j < n - 1, j > down))
             def _():
-                rs_in(t, 1, k).wait_recv()
-                rs_s[t, 1, k] = (prod[down] + rs_r[t, 1, k].astype(jnp.float32)).astype(jnp.bfloat16)
-                rs_copy(t, 1, k).start()
+                for h in range(2):
+                    at = halves[h]
+                    rs_in(t, 1, k, h).wait_recv()
+                    total = prod[down, at] + rs_r[t, 1, k, at].astype(jnp.float32)
+                    rs_s[t, 1, k, at] = total.astype(jnp.bfloat16)
+                    rs_copy(t, 1, k, h).start()
 
             for side in range(2):
                 block = j - 1 - k if side == 0 else j + 1 + k
                 pl.when(arrives(side, k))(lambda block=block: take(block))
+            for h in range(2):
+                for side in range(2):
+                    if k > 0:
+                        line_recv(*sts, t + 1, side, k - 1, h, more)
+                    line_send(*sts, t + 1, side, k, h, more)
 
         factor = lax.rsqrt(ssq[:, :1] / extent + EPSILON) * (1.0 / root)
         fwd[t] = (xg[t, j].astype(jnp.float32) + acc[...] * factor).astype(jnp.bfloat16)
@@ -320,12 +339,14 @@
 
         @pl.when(j > 0)
         def _():
-            rs_in(t, 0, n - 1 - j).wait_recv()
+            for h in range(2):
+                rs_in(t, 0, n - 1 - j, h).wait_recv()
             prod[j] += rs_r[t, 0, n - 1 - j].astype(jnp.float32)
 
         @pl.when(j < n - 1)
         def _():
-            rs_in(t, 1, j).wait_recv()
+            for h in range(2):
+                rs_in(t, 1, j, h).wait_recv()
             prod[j] += rs_r[t, 1, j].astype(jnp.float32)
 
         inner = inm[t]
@@ -341,8 +362,9 @@
         ).astype(jnp.bfloat16)
         pl.when(both(more, s > 0))(lambda: bwd_copy(t).start())
 
-        for side in range(2):
-            line_recv(*sts, t + 1, side, n - 2, more)
+        for h in range(2):
+            for side in range(2):
+                line_recv(*sts, t + 1, side, n - 2, h, more)
         pl.when(more)(lambda: stash_finish(t + 1))
         return carry
 
@@ -361,11 +383,12 @@
         for q in range(1, n):
             inner_copy(t, q).wait_send()
         for k in range(n - 1):
-            for side in range(2):
-                line_sent(*xs, t, side, k)
-                line_sent(*sts, t, side, k)
-            pl.when(j < n - 1 - k)(lambda: rs_copy(t, 0, k).wait_send())
-            pl.when(j > k)(lambda: rs_copy(t, 1, k).wait_send())
+            for h in range(2):
+                for side in range(2):
+                    line_sent(*xs, t, side, k, h)
+                    line_sent(*sts, t, side, k, h)
+                pl.when(j < n - 1 - k)(lambda: rs_copy(t, 0, k, h).wait_send())
+                pl.when(j > k)(lambda: rs_copy(t, 1, k, h).wait_send())
         pl.when(both(t < ticks - 1, s < sections - 1))(lambda: fwd_copy(t).wait_send())
         pl.when(both(t < ticks - 1, s > 0))(lambda: bwd_copy(t).wait_send())
         return carry
@@ -420,12 +443,12 @@
             pltpu.VMEM((ticks, rows, LANES), f32),
             pltpu.VMEM((ticks, n - 1, rows, LANES), f32),
             dma((6,)),
-            dma((ticks, 2, n - 1)),
-            dma((ticks, 2, n - 1)),
-            dma((ticks, 2, n - 1)),
-            dma((ticks, 2, n - 1)),
-            dma((ticks, 2, n - 1)),
-            dma((ticks, 2, n - 1)),
+            dma((ticks, 2, n - 1, 2)),
+            dma((ticks, 2, n - 1, 2)),
+            dma((ticks, 2, n - 1, 2)),
+            dma((ticks, 2, n - 1, 2)),
+            dma((ticks, 2, n - 1, 2)),
+            dma((ticks, 2, n - 1, 2)),
             dma((ticks,)),
             dma((ticks,)),
             dma((ticks,)),

time: 167 us -> 162 us (0.970)
  Pallas kernels: 157 us -> 152 us
    pallas_call x1, Pallas kernels: 145 us -> 141 us  [body(): pl.pallas_call(functools.partial(window_kernel, n, dp, sections), out_sha...]
where the time goes in v2:
time: 162 us
  Pallas kernels  152 us (94%)
  local copies, waits for them, and re-layouts  8.74 us (5%)
    pallas_call x1, Pallas kernels, body(): pl.pallas_call(functools.partial(window_kernel, n, dp, sections), out_sha...  141 us
    pallas_call x1, Pallas kernels, body(): pl.pallas_call(update_kernel, out_shape=(jax.ShapeDtypeStruct((own_rows,...  11.4 us
    unnamed x16, local copies, waits for them, and re-layouts  8.74 us

profile of v2, /device:TPU:0, one launch (start us, length us, event | category | flops | bytes accessed | tf_op | source)
XLA Modules:
  0.0 161.6 jit_solution(5244048560855838232)
XLA Ops:
  0.6 0.0 copy-start.2
  0.6 1.0 copy-done.2
  1.7 0.0 copy-start.3
  1.7 1.0 copy-done.3
  2.7 0.0 copy-start.4
  2.7 1.0 copy-done.4
  3.7 0.0 copy-start.5
  3.7 0.9 copy-done.5
  4.6 0.0 copy-start.6
  4.6 0.9 copy-done.6
  5.5 140.7 %window.1 = (bf16[4,64,1024]{2,1,0:T(8,128)(2,1)S(1)}, bf16[4,64,1024]{2,1,0:T(8,128)(2,1)S(1)}, bf16[2,2,4,64,1024]{4,3,2,1,0:T(8,128)(2,1)S(1)}, bf16[2,4,64,1024]{3,2,1,0:T(8,128)(2,1)S(1)}) custom-call(bf16[4,1024,1024]{2,1,0:T(8,128)(2,1)} %bitcast.23, bf16[64,1024]{1,0:T(8,128)(2,1)S(1)} %bitcast.21, bf16[3,64,1024]{2,1,0:T(8,128)(2,1)S(1)} %bitcast.19, ...), custom_call_target="tpu_custom_call" | custom-call | tf_op jit(solution)/shard_map/window/pallas_call | solution.py:420
  146.2 0.0 copy-start
  146.2 1.3 copy-done
  147.6 0.0 copy-start.1
  147.6 1.0 copy-done.1
  148.6 11.4 %update.1 = (bf16[2048,1024]{1,0:T(8,128)(2,1)}, bf16[2048,1024]{1,0:T(8,128)(2,1)}) custom-call(bf16[2,512,1024]{2,1,0:T(8,128)(2,1)} %bitcast.14, bf16[512,1024]{1,0:T(8,128)(2,1)} %bitcast.15, bf16[2048,1024]{1,0:T(8,128)(2,1)} %bitcast.24, bf16[2048,1024]{1,0:T(8,128)(2,1)} %bitcast.25), custom_call_target="tpu_custom_call" | custom-call | tf_op jit(solution)/shard_map/update/pallas_call | solution.py:481
  160.0 0.8 copy.14
  160.8 0.8 copy.15
Async XLA Ops:
  0.6 1.0 copy-start.2
  1.7 1.0 copy-start.3
  2.7 1.0 copy-start.4
  3.7 0.9 copy-start.5
  4.6 0.9 copy-start.6
  146.2 1.3 copy-start
  147.6 1.0 copy-start.1
